TPU v7x, 32 devices: a whole 2x2x4 slice. The times are simulated.
32 devices in a mesh: seq: 2 (over y), dp: 16 (over z, x, core).
Axes of the slice: x: 2, y: 2, z: 4, core: 2. Of those that a mesh axis runs over, the one named last changes fastest.
Arguments:
- inputs: bfloat16 [16, 2, 1024, 768], P('dp', None, 'seq'), may hold values from -6 to 6
- query_weight: bfloat16 [768, 768], P(('seq', 'dp')), may hold values from -0.21875 to 0.21875
- key_weight: bfloat16 [768, 768], P(('seq', 'dp')), may hold values from -0.21875 to 0.21875
- value_weight: bfloat16 [768, 768], P(('seq', 'dp')), may hold values from -0.21875 to 0.21875
- query_bias: bfloat16 [768], P(('seq', 'dp')), may hold values from -3 to 3
- value_bias: bfloat16 [768], P(('seq', 'dp')), may hold values from -3 to 3
- output_weight: bfloat16 [768, 768], P(('seq', 'dp')), may hold values from -2.5 to 2.5
- output_bias: bfloat16 [768], P(('seq', 'dp')), may hold values from -3 to 3
- first_gain: bfloat16 [768], P(('seq', 'dp')), may hold values from 0.099609375 to 1.8984375
- first_shift: bfloat16 [768], P(('seq', 'dp')), may hold values from -3 to 3
- inner_weight: bfloat16 [768, 3072], P(('seq', 'dp')), may hold values from -0.21875 to 0.21875
- inner_bias: bfloat16 [3072], P(('seq', 'dp')), may hold values from -3 to 3
- outer_weight: bfloat16 [3072, 768], P(('seq', 'dp')), may hold values from -0.109375 to 0.109375
- outer_bias: bfloat16 [768], P(('seq', 'dp')), may hold values from -3 to 3
- second_gain: bfloat16 [768], P(('seq', 'dp')), may hold values from 0.099609375 to 1.8984375
- second_shift: bfloat16 [768], P(('seq', 'dp')), may hold values from -3 to 3
- prefix: int32 [16, 2], P('dp'), may hold values from 102 to 512, as said below
- cotangent: bfloat16 [16, 2, 1024, 768], P('dp', None, 'seq'), may hold values from -6 to 6
Outputs:
- outputs: bfloat16 [16, 2, 1024, 768], P('dp', None, 'seq')
- input_grad: float32 [16, 2, 1024, 768], P('dp', None, 'seq')
- grad_query_weight: float32 [768, 768], P(('seq', 'dp'))
- grad_key_weight: float32 [768, 768], P(('seq', 'dp'))
- grad_value_weight: float32 [768, 768], P(('seq', 'dp'))
- grad_query_bias: float32 [768], P(('seq', 'dp'))
- grad_value_bias: float32 [768], P(('seq', 'dp'))
- grad_output_weight: float32 [768, 768], P(('seq', 'dp'))
- grad_output_bias: float32 [768], P(('seq', 'dp'))
- grad_first_gain: float32 [768], P(('seq', 'dp'))
- grad_first_shift: float32 [768], P(('seq', 'dp'))
- grad_inner_weight: float32 [768, 3072], P(('seq', 'dp'))
- grad_inner_bias: float32 [3072], P(('seq', 'dp'))
- grad_outer_weight: float32 [3072, 768], P(('seq', 'dp'))
- grad_outer_bias: float32 [768], P(('seq', 'dp'))
- grad_second_gain: float32 [768], P(('seq', 'dp'))
- grad_second_shift: float32 [768], P(('seq', 'dp'))
Inputs may be any that keep to these rules, and one draw needn't show every extreme that they name: `prefix`: the number of leading tokens of each sequence that attend to one another both ways; some sequence has 512 and some 1024 // 10.
All inputs are finite; a program needn't handle non-finite values.
Results may differ from a plain program's by a relative error of at most 0.017.
Values may be sent and summed in bfloat16 or wider, within the bound.
A program may use at most 384 MiB of HBM per device.

v0:
```python
import jax
import jax.numpy as jnp
from jax import lax
from jax.sharding import PartitionSpec as P

HEADS = 12
HEAD_DIM = 64
EPS = 1e-05
FAR = 1 << 20
BOTH = ("seq", "dp")
F32 = jnp.float32
BF16 = jnp.bfloat16


def dot(a, b):
    return jnp.dot(a, b, preferred_element_type=F32)


def dot_t(a, b):
    return lax.dot_general(a, b, (((1,), (1,)), ((), ())), preferred_element_type=F32)


def t_dot(a, b):
    return lax.dot_general(a, b, (((0,), (0,)), ((), ())), preferred_element_type=F32)


def norm_parts(v):
    center = v - jnp.mean(v, axis=-1, keepdims=True)
    inv = lax.rsqrt(jnp.mean(center * center, axis=-1, keepdims=True) + EPS)
    return (center * inv, inv)


def norm_grad(grad, unit, inv, gain):
    g = grad * gain
    mean_g = jnp.mean(g, axis=-1, keepdims=True)
    mean_gu = jnp.mean(g * unit, axis=-1, keepdims=True)
    return inv * (g - mean_g - unit * mean_gu)


def heads_of(v):
    return v.reshape(v.shape[0], HEADS, HEAD_DIM)


def attend(q, k, v, key_pos, limit):
    scores = (
        jnp.einsum("qhd,khd->hqk", heads_of(q), heads_of(k), preferred_element_type=F32) * 0.125
    )
    scores = jnp.where((key_pos[None, :] <= limit[:, None])[None], scores, -1e30)
    top = jnp.max(scores, axis=-1, keepdims=True)
    lse = top[..., 0] + jnp.log(jnp.sum(jnp.exp(scores - top), axis=-1))
    probs = jnp.exp(scores - lse[..., None])
    low = probs.astype(BF16)
    mixed = jnp.einsum("hqk,khd->qhd", low, heads_of(v), preferred_element_type=F32)
    return (mixed.reshape(q.shape).astype(BF16), (probs, low))


def attend_back(saved, q, k, v, mixed, grad):
    probs, low = saved
    grad_h = heads_of(grad)
    grad_probs = jnp.einsum("qhd,khd->hqk", grad_h, heads_of(v), preferred_element_type=F32)
    row_dot = jnp.sum(grad_probs * probs, axis=-1, keepdims=True)
    grad_scores = (probs * (grad_probs - row_dot)).astype(BF16)
    gq = jnp.einsum("hqk,khd->qhd", grad_scores, heads_of(k), preferred_element_type=F32) * 0.125
    gk = jnp.einsum("hqk,qhd->khd", grad_scores, heads_of(q), preferred_element_type=F32) * 0.125
    gv = jnp.einsum("hqk,qhd->khd", low, grad_h, preferred_element_type=F32)
    return (
        gq.reshape(q.shape).astype(BF16),
        gk.reshape(k.shape).astype(BF16),
        gv.reshape(v.shape).astype(BF16),
    )


def on_device(
    inputs,
    query_weight,
    key_weight,
    value_weight,
    query_bias,
    value_bias,
    output_weight,
    output_bias,
    first_gain,
    first_shift,
    inner_weight,
    inner_bias,
    outer_weight,
    outer_bias,
    second_gain,
    second_shift,
    prefix,
    cotangent,
):
    micros, rows, width = inputs.shape[1:]
    own = query_weight.shape[0]
    hidden_width = inner_weight.shape[1]
    per = hidden_width // width
    seqs = lax.axis_size("seq")
    seq_at = lax.axis_index("seq")
    first_pos = seq_at * rows
    x = inputs[0]
    flat_x = x.reshape(micros * rows, width)
    row_pos = first_pos + jnp.arange(rows, dtype=jnp.int32)
    if seqs == 2:
        before = lax.ppermute(x, "seq", [(0, 1)])
        key_x = jnp.concatenate([x, before], axis=1)
        key_pos = jnp.concatenate(
            [row_pos, jnp.where(seq_at == 1, jnp.arange(rows, dtype=jnp.int32), FAR)]
        )
    else:
        key_x = lax.all_gather(x, "seq", axis=1, tiled=True)
        key_pos = jnp.arange(seqs * rows, dtype=jnp.int32)
    total_rows = key_x.shape[1]
    flat_key_x = key_x.reshape(micros * total_rows, width)
    vectors = (
        query_bias,
        value_bias,
        output_bias,
        first_gain,
        first_shift,
        outer_bias,
        second_gain,
        second_shift,
    )
    small = jnp.concatenate([jnp.stack(vectors, axis=1), inner_bias.reshape(own, per)], axis=1)
    small_count = small.shape[1]
    small = jnp.pad(small, ((0, 0), (0, 128 - small_count)))
    first_pack = lax.all_gather(
        jnp.concatenate([query_weight, key_weight, value_weight, small], axis=1),
        BOTH,
        axis=0,
        tiled=True,
    )
    second_pack = lax.all_gather(
        jnp.concatenate([output_weight, inner_weight], axis=1), BOTH, axis=0, tiled=True
    )
    full_outer = lax.all_gather(outer_weight, BOTH, axis=0, tiled=True)
    full_query = first_pack[:, :width]
    full_kv = first_pack[:, width : 3 * width]
    small_all = first_pack[:, 3 * width : 3 * width + small_count].astype(F32)
    qb, vb, ob, fg, fs, ub, sg, ss = [small_all[:, i] for i in range(8)]
    ib = small_all[:, 8:].reshape(hidden_width)
    full_output = second_pack[:, :width]
    full_inner = second_pack[:, width:]
    queries = (dot(flat_x, full_query) + qb).astype(BF16).reshape(micros, rows, width)
    kv_bias = jnp.concatenate([jnp.zeros_like(vb), vb])
    keys_values = (
        (dot(flat_key_x, full_kv) + kv_bias).astype(BF16).reshape(micros, total_rows, 2 * width)
    )
    keys, values = (keys_values[..., :width], keys_values[..., width:])
    mixed_parts, saved = ([], [])
    for m in range(micros):
        limit = jnp.maximum(row_pos, prefix[0, m] - 1)
        mixed_m, saved_m = attend(queries[m], keys[m], values[m], key_pos, limit)
        mixed_parts.append(mixed_m)
        saved.append(saved_m)
    mixed = jnp.concatenate(mixed_parts, axis=0)
    unit1, inv1 = norm_parts(flat_x.astype(F32) + dot(mixed, full_output) + ob)
    middle = unit1 * fg + fs
    middle_low = middle.astype(BF16)
    inner = dot(middle_low, full_inner) + ib
    half_cdf = 0.5 * (1.0 + lax.erf(inner * 0.5**0.5))
    hidden = (inner * half_cdf).astype(BF16)
    slope = half_cdf + inner * jnp.exp(-0.5 * inner * inner) * 0.3989422804014327
    unit2, inv2 = norm_parts(middle + dot(hidden, full_outer) + ub)
    result = (unit2 * sg + ss).astype(BF16)
    cot = cotangent[0].reshape(micros * rows, width).astype(F32)
    g_sgain = jnp.sum(cot * unit2, axis=0)
    g_sshift = jnp.sum(cot, axis=0)
    grad_mid2 = norm_grad(cot, unit2, inv2, sg)
    grad_outer = grad_mid2.astype(BF16)
    g_ubias = jnp.sum(grad_outer.astype(F32), axis=0)
    g_outer = t_dot(hidden, grad_outer).astype(BF16)
    own_outer = lax.psum_scatter(g_outer, BOTH, scatter_dimension=0, tiled=True).astype(F32)
    grad_hidden = dot_t(grad_outer, full_outer).astype(BF16)
    grad_inner = (grad_hidden.astype(F32) * slope).astype(BF16)
    g_ibias = jnp.sum(grad_inner.astype(F32), axis=0)
    g_inner = t_dot(middle_low, grad_inner)
    grad_middle = grad_mid2 + dot_t(grad_inner, full_inner)
    g_fgain = jnp.sum(grad_middle * unit1, axis=0)
    g_fshift = jnp.sum(grad_middle, axis=0)
    grad_sum1 = norm_grad(grad_middle, unit1, inv1, fg)
    grad_branch = grad_sum1.astype(BF16)
    g_obias = jnp.sum(grad_branch.astype(F32), axis=0)
    g_output = t_dot(mixed, grad_branch)
    own_second = lax.psum_scatter(
        jnp.concatenate([g_output, g_inner], axis=1).astype(BF16),
        BOTH,
        scatter_dimension=0,
        tiled=True,
    ).astype(F32)
    grad_mixed = dot_t(grad_branch, full_output).astype(BF16).reshape(micros, rows, width)
    gq_parts, gk_parts, gv_parts = ([], [], [])
    for m in range(micros):
        gq, gk, gv = attend_back(
            saved[m], queries[m], keys[m], values[m], mixed_parts[m], grad_mixed[m]
        )
        gq_parts.append(gq)
        gk_parts.append(gk)
        gv_parts.append(gv)
    grad_q = jnp.concatenate(gq_parts, axis=0)
    grad_kv = jnp.concatenate([jnp.stack(gk_parts), jnp.stack(gv_parts)], axis=-1)
    flat_kv = grad_kv.reshape(micros * total_rows, 2 * width)
    g_qbias = jnp.sum(grad_q.astype(F32), axis=0)
    g_vbias = jnp.sum(flat_kv[:, width:].astype(F32), axis=0)
    g_query = t_dot(flat_x, grad_q)
    g_kv = t_dot(flat_key_x, flat_kv)
    g_small = jnp.concatenate(
        [
            jnp.stack(
                [g_qbias, g_vbias, g_obias, g_fgain, g_fshift, g_ubias, g_sgain, g_sshift], axis=1
            ),
            g_ibias.reshape(width, per),
        ],
        axis=1,
    )
    g_small = jnp.pad(g_small, ((0, 0), (0, 128 - small_count)))
    own_first = lax.psum_scatter(
        jnp.concatenate([g_query, g_kv, g_small], axis=1).astype(BF16),
        BOTH,
        scatter_dimension=0,
        tiled=True,
    ).astype(F32)
    via_kv = dot_t(flat_kv, full_kv).reshape(micros, total_rows, width)
    grad_x = (grad_sum1 + dot_t(grad_q, full_query)).reshape(micros, rows, width)
    if seqs == 2:
        grad_x = grad_x + via_kv[:, :rows]
        grad_x = grad_x + lax.ppermute(via_kv[:, rows:].astype(BF16), "seq", [(1, 0)]).astype(F32)
    else:
        grad_x = grad_x + lax.psum_scatter(via_kv, "seq", scatter_dimension=1, tiled=True)
    vec = own_first[:, 3 * width : 3 * width + small_count]
    v_of = [vec[:, i] for i in range(8)]
    outputs = result.reshape(micros, rows, width)[None]
    return (
        outputs,
        grad_x[None],
        own_first[:, :width],
        own_first[:, width : 2 * width],
        own_first[:, 2 * width : 3 * width],
        v_of[0],
        v_of[1],
        own_second[:, :width],
        v_of[2],
        v_of[3],
        v_of[4],
        own_second[:, width:],
        vec[:, 8:].reshape(own * per),
        own_outer,
        v_of[5],
        v_of[6],
        v_of[7],
    )


def solution(mesh):
    act = P("dp", None, "seq", None)
    mat = P(BOTH, None)
    vec = P(BOTH)
    params = (mat, mat, mat, vec, vec, mat, vec, vec, vec, mat, vec, mat, vec, vec, vec)
    return jax.shard_map(
        on_device,
        mesh=mesh,
        in_specs=(act,) + params + (P("dp", None), act),
        out_specs=(act, act) + params,
        check_vma=False,
    )
```

profile of v0, /device:TPU:0, one launch (start us, length us, event | category | flops | bytes accessed | tf_op | source)
XLA Modules:
  0.0 761.0 jit_solution(18443517237392561761)
XLA Ops:
  19.2 6.1 collective-permute-start
  30.0 30.2 %collective-permute-done = bf16[2,512,768]{1,2,0:T(8,128)(2,1)} collective-permute-done((bf16[2,512,768]{1,2,0:T(8,128)(2,1)S(1)}, bf16[2,512,768]{1,2,0:T(8,128)(2,1)}, u32[]{:S(2)}, u32[]{:S(2)}) %collective-permute-start) | collective-permute-done | bytes 1572896 | tf_op jit(solution)/shard_map/ppermute | solution.py:104
  68.5 11.6 %all-gather.4.cloned.1.call-done = bf16[768,2432]{1,0:T(8,128)(2,1)} async-done(((bf16[24,2432]{1,0:T(8,128)(2,1)}), bf16[768,2432]{1,0:T(8,128)(2,1)}) %all-gather.4.cloned.1.call-update) | async-done | bytes 3735568 | tf_op jit(solution)/shard_map/all_gather | solution.py:127
  87.6 5.4 add_convert_fusion
  97.6 12.8 %fusion.1 = (f32[12,512]{1,0:T(8,128)S(1)}, f32[12,512,1024]{2,1,0:T(8,128)}) fusion(pred[512,1024]{1,0:T(8,128)(4,1)} %get-tuple-element.56, bf16[512,12,64]{0,2,1:T(8,128)(2,1)} %bitcast.115, bf16[1024,12,64]{0,2,1:T(8,128)(2,1)S(1)} %bitcast.111), kind=kOutput, calls=%fused_computation.11 | convolution fusion | flops 824174592 | bytes 28073984 | tf_op jit(solution)/shard_map/qhd,khd->hqk/dot_general | solution.py:46
  110.4 12.5 %exponential_reduce_fusion = f32[12,512]{1,0:T(8,128)} fusion(f32[12,512,1024]{2,1,0:T(8,128)} %get-tuple-element.60, f32[12,512]{1,0:T(8,128)S(1)} %get-tuple-element.59, pred[512,1024]{1,0:T(8,128)(4,1)S(1)} %copy-done.3), kind=kLoop, calls=%fused_computation.5 | loop fusion | flops 25159680 | bytes 25739264 | tf_op jit(solution)/shard_map/reduce_sum | solution.py:50
  130.8 12.4 %fusion = (f32[12,512]{1,0:T(8,128)S(1)}, f32[12,512,1024]{2,1,0:T(8,128)}) fusion(pred[512,1024]{1,0:T(8,128)(4,1)} %get-tuple-element.55, bf16[512,12,64]{0,2,1:T(8,128)(2,1)} %bitcast.117, bf16[1024,12,64]{0,2,1:T(8,128)(2,1)S(1)} %bitcast.113), kind=kOutput, calls=%fused_computation.10 | convolution fusion | flops 824174592 | bytes 28073984 | tf_op jit(solution)/shard_map/qhd,khd->hqk/dot_general | solution.py:46
  143.2 12.2 %exponential_reduce_fusion.1 = f32[12,512]{1,0:T(8,128)S(1)} fusion(f32[12,512,1024]{2,1,0:T(8,128)} %get-tuple-element.62, f32[12,512]{1,0:T(8,128)S(1)} %get-tuple-element.61, pred[512,1024]{1,0:T(8,128)(4,1)S(1)} %copy-done.7), kind=kLoop, calls=%fused_computation.8 | loop fusion | flops 25159680 | bytes 25739264 | tf_op jit(solution)/shard_map/reduce_sum | solution.py:50
  155.4 12.2 %convolution_convert_fusion.7 = bf16[12,64,512]{2,1,0:T(8,128)(2,1)} fusion(bf16[1024,12,64]{0,2,1:T(8,128)(2,1)S(1)} %bitcast.121, f32[12,512,1024]{2,1,0:T(8,128)} %get-tuple-element.60, f32[12,512]{1,0:T(8,128)S(1)} %log_add_fusion, pred[512,1024]{1,0:T(8,128)(4,1)S(1)} %copy-done.4), kind=kOutput, calls=%fused_computation.85 | convolution fusion | flops 830865408 | bytes 28073984 | tf_op jit(solution)/shard_map/hqk,khd->qhd/dot_general | solution.py:53
  167.6 11.9 %convolution_convert_fusion.8 = bf16[12,64,512]{2,1,0:T(8,128)(2,1)} fusion(bf16[1024,12,64]{0,2,1:T(8,128)(2,1)S(1)} %bitcast.123, f32[12,512,1024]{2,1,0:T(8,128)} %get-tuple-element.62, f32[12,512]{1,0:T(8,128)S(1)} %log_add_fusion.1, pred[512,1024]{1,0:T(8,128)(4,1)S(1)} %copy-done.7), kind=kOutput, calls=%fused_computation.86 | convolution fusion | flops 830865408 | bytes 28073984 | tf_op jit(solution)/shard_map/hqk,khd->qhd/dot_general | solution.py:53
  185.4 10.1 %multiply_convert_fusion.2 = (bf16[1024,3072]{1,0:T(8,128)(2,1)}, f32[1024,3072]{1,0:T(8,128)}) fusion(f32[3072]{0:T(1024)S(1)} %add.172, bf16[768,3840]{1,0:T(8,128)(2,1)S(1)} %bitcast.155, f32[1024,768]{1,0:T(8,128)S(1)} %get-tuple-element.64, f32[768]{0:T(1024)S(1)} %copy-done.50, f32[768]{0:T(1024)S(1)} %get-tuple-element.27, ...), kind=kOutput, calls=%fused_computation.21 | convolution fusion | flops 4854644736 | bytes 26767360 | tf_op jit(solution)/shard_map/dot_general | solution.py:16
  195.5 19.7 %all-gather.8.cloned.1.call-done = bf16[3072,768]{1,0:T(8,128)(2,1)} async-done(((bf16[96,768]{1,0:T(8,128)(2,1)}), bf16[3072,768]{1,0:T(8,128)(2,1)}) %all-gather.8.cloned.1.call-update) | async-done | bytes 4718608 | tf_op jit(solution)/shard_map/all_gather | solution.py:136
  215.2 9.3 %fusion.72 = (f32[1024]{0:T(1024)S(1)}, f32[1024,768]{1,0:T(8,128)S(1)}) fusion(f32[768]{0:T(1024)S(1)} %copy-done.52, bf16[1024,3072]{1,0:T(8,128)(2,1)} %get-tuple-element.65, bf16[3072,768]{1,0:T(8,128)(2,1)} %all-gather.8.cloned.1.call-done, f32[768]{0:T(1024)S(1)} %copy-done.50, f32[768]{0:T(1024)S(1)} %get-tuple-element.27, ...), kind=kOutput, calls=%fused_computation.155 | convolution fusion | flops 4837342208 | bytes 17323008 | tf_op jit(solution)/shard_map/dot_general | solution.py:16
  230.3 14.9 %fusion.73 = (bf16[3072]{0:T(1024)(128)(2,1)}, bf16[1024,3072]{1,0:T(8,128)(2,1)}) fusion(f32[1024,3072]{1,0:T(8,128)} %get-tuple-element.66, f32[3072]{0:T(1024)S(1)} %add.172, bf16[3072,768]{1,0:T(8,128)(2,1)S(1)} %bitcast.159, f32[1024,768]{1,0:T(8,128)S(1)} %get-tuple-element.40), kind=kOutput, calls=%fused_computation.156 | convolution fusion | flops 4876661760 | bytes 26757120 | tf_op jit(solution)/shard_map/dot_general | solution.py:20
  245.2 8.8 %multiply_reduce_fusion.2 = (bf16[768]{0:T(1024)(128)(2,1)}, f32[1024]{0:T(1024)S(1)}, f32[1024]{0:T(1024)S(1)}, bf16[768]{0:T(1024)(128)(2,1)}, f32[1024,768]{1,0:T(8,128)S(1)}) fusion(f32[1024,768]{1,0:T(8,128)S(1)} %copy-done.10, f32[1024]{0:T(1024)S(1)} %add_rsqrt_fusion.1, f32[1024]{0:T(1024)S(1)} %broadcast_multiply_fusion.4, ...), kind=kOutput, calls=%fused_computation.52 | convolution fusion | flops 4839698432 | bytes 20470784 | tf_op jit(solution)/shard_map/dot_general | solution.py:20
  258.6 12.7 %convolution_convert_fusion.3 = bf16[12,64,1024]{2,1,0:T(8,128)(2,1)} fusion(bf16[512,12,64]{0,2,1:T(8,128)(2,1)S(1)} %bitcast.133, f32[12,512,1024]{2,1,0:T(8,128)} %get-tuple-element.62, f32[12,512]{1,0:T(8,128)S(1)} %copy-done.40, pred[512,1024]{1,0:T(8,128)(4,1)S(1)} %copy-done.8), kind=kOutput, calls=%fused_computation.75 | convolution fusion | flops 831258624 | bytes 28073984 | tf_op jit(solution)/shard_map/hqk,qhd->khd/dot_general | solution.py:65
  271.4 21.9 %multiply_reduce_fusion.1 = (f32[12,512]{1,0:T(8,128)}, f32[12,512,1024]{2,1,0:T(8,128)}) fusion(f32[12,512,1024]{2,1,0:T(8,128)} %get-tuple-element.62, f32[12,512]{1,0:T(8,128)S(1)} %copy-done.40, pred[512,1024]{1,0:T(8,128)(4,1)S(1)} %copy-done.8, bf16[512,12,64]{0,2,1:T(8,128)(2,1)S(1)} %bitcast.134, bf16[1024,12,64]{0,2,1:T(8,128)(2,1)S(1)} %bitcast.124), kind=kOutput, calls=%fused_computation.3 | convolution fusion | flops 836757504 | bytes 53264384 | tf_op jit(solution)/shard_map/qhd,khd->hqk/dot_general | solution.py:60
  293.3 17.5 %multiply_convert_fusion.1 = bf16[12,512,1024]{2,1,0:T(8,128)(2,1)S(1)} fusion(f32[12,512,1024]{2,1,0:T(8,128)} %get-tuple-element.73, f32[12,512,1024]{2,1,0:T(8,128)} %get-tuple-element.62, f32[12,512]{1,0:T(8,128)} %get-tuple-element.72, f32[12,512]{1,0:T(8,128)} %copy-done.39, pred[512,1024]{1,0:T(8,128)(4,1)} %get-tuple-element.55), kind=kLoop, calls=%fused_computation.2 | loop fusion | flops 37748736 | bytes 63488000 | tf_op jit(solution)/shard_map/convert_element_type | solution.py:62
  310.8 6.2 bitcast_reduce_fusion.1
  321.8 12.8 %convolution_convert_fusion.2 = bf16[12,64,1024]{2,1,0:T(8,128)(2,1)} fusion(bf16[512,12,64]{0,2,1:T(8,128)(2,1)S(1)} %bitcast.131, f32[12,512,1024]{2,1,0:T(8,128)} %get-tuple-element.60, f32[12,512]{1,0:T(8,128)S(1)} %copy-done.38, pred[512,1024]{1,0:T(8,128)(4,1)S(1)} %copy-done.5), kind=kOutput, calls=%fused_computation.74 | convolution fusion | flops 831258624 | bytes 28073984 | tf_op jit(solution)/shard_map/hqk,qhd->khd/dot_general | solution.py:65
  334.6 21.3 %multiply_reduce_fusion = (f32[12,512]{1,0:T(8,128)S(1)}, f32[12,512,1024]{2,1,0:T(8,128)}) fusion(f32[12,512,1024]{2,1,0:T(8,128)} %get-tuple-element.60, f32[12,512]{1,0:T(8,128)S(1)} %copy-done.38, pred[512,1024]{1,0:T(8,128)(4,1)S(1)} %copy-done.6, bf16[512,12,64]{0,2,1:T(8,128)(2,1)S(1)} %bitcast.132, bf16[1024,12,64]{0,2,1:T(8,128)(2,1)S(1)} %bitcast.122), kind=kOutput, calls=%fused_computation.1 | convolution fusion | flops 836757504 | bytes 53264384 | tf_op jit(solution)/shard_map/qhd,khd->hqk/dot_general | solution.py:60
  355.9 17.6 %multiply_convert_fusion = bf16[12,512,1024]{2,1,0:T(8,128)(2,1)S(1)} fusion(f32[12,512,1024]{2,1,0:T(8,128)} %get-tuple-element.71, f32[12,512,1024]{2,1,0:T(8,128)} %get-tuple-element.60, f32[12,512]{1,0:T(8,128)S(1)} %get-tuple-element.70, f32[12,512]{1,0:T(8,128)S(1)} %copy-done.38, pred[512,1024]{1,0:T(8,128)(4,1)} %get-tuple-element.56), kind=kLoop, calls=%fused_computation | loop fusion | flops 37748736 | bytes 63488000 | tf_op jit(solution)/shard_map/convert_element_type | solution.py:62
  373.6 6.2 bitcast_reduce_fusion
  412.0 8.0 %bitcast_convert_fusion = bf16[768,1536]{1,0:T(8,128)(2,1)S(1)} fusion(bf16[2,512,768]{1,2,0:T(8,128)(2,1)} %collective-permute-done, bf16[2,512,768]{1,2,0:T(8,128)(2,1)} %bitcast.128, bf16[1,1024,768]{2,1,0:T(8,128)(2,1)S(1)} %copy-done.17, bf16[1,1024,768]{2,1,0:T(8,128)(2,1)S(1)} %copy-done.19, bf16[1,1024,768]{2,1,0:T(8,128)(2,1)} %copy.119, ...), kind=kOutput, calls=%fused_computation.30 | convolution fusion | flops 4864475136 | bytes 11796480 | tf_op jit(solution)/shard_map/dot_general | solution.py:24
  423.9 9.9 %convolution_convert_fusion = bf16[3072,768]{1,0:T(8,128)(2,1)} fusion(bf16[1024,3072]{1,0:T(8,128)(2,1)} %get-tuple-element.65, f32[1024,768]{1,0:T(8,128)S(1)} %copy-done.28), kind=kOutput, calls=%fused_computation.28 | convolution fusion | flops 4834983936 | bytes 14155776 | tf_op jit(solution)/shard_map/dot_general | solution.py:24
  433.9 5.1 convolution_convert_fusion.5
  441.6 8.7 %convolution_convert_fusion.1 = bf16[768,3072]{1,0:T(8,128)(2,1)S(1)} fusion(bf16[1024,3072]{1,0:T(8,128)(2,1)} %get-tuple-element.79, f32[1024,768]{1,0:T(8,128)S(1)} %copy-done.11, f32[768]{0:T(1024)S(1)} %copy-done.51, f32[768]{0:T(1024)S(1)} %get-tuple-element.27, f32[1024]{0:T(1024)S(1)} %add_rsqrt_fusion.1, f32[1024]{0:T(1024)S(1)} %broadcast_multiply_fusion.4), kind=kOutput, calls=%fused_computation.29 | convolution fusion | flops 4838129664 | bytes 14170112 | tf_op jit(solution)/shard_map/dot_general | solution.py:24
  455.2 8.0 %fusion.26 = f32[2,1024,768]{2,1,0:T(8,128)S(1)} fusion(bf16[768,2432]{1,0:T(8,128)(2,1)} %all-gather.4.cloned.1.call-done, bf16[1,1024,768]{2,1,0:T(8,128)(2,1)S(1)} %copy-done.18, bf16[1,1024,768]{2,1,0:T(8,128)(2,1)S(1)} %copy-done.20, bf16[1,1024,768]{2,1,0:T(8,128)(2,1)} %copy.119, bf16[1,1024,768]{2,1,0:T(8,128)(2,1)} %copy.118), kind=kOutput, calls=%fused_computation.68 | convolution fusion | flops 4857004032 | bytes 14942208 | tf_op jit(solution)/shard_map/dot_general | solution.py:20
  467.4 37.9 %collective-permute-done.1 = bf16[2,512,768]{2,1,0:T(8,128)(2,1)S(1)} collective-permute-done((bf16[2,512,768]{2,1,0:T(8,128)(2,1)S(1)}, bf16[2,512,768]{2,1,0:T(8,128)(2,1)S(1)}, u32[]{:S(2)}, u32[]{:S(2)}) %collective-permute-start.1) | collective-permute-done | bytes 1572896 | tf_op jit(solution)/shard_map/ppermute | solution.py:227
  507.7 13.3 %reduce-scatter.10.cloned.1.call-done = bf16[24,2432]{1,0:T(8,128)(2,1)} async-done(((bf16[768,2432]{1,0:T(8,128)(2,1)}), bf16[24,2432]{1,0:T(8,128)(2,1)}) %reduce-scatter.10.cloned.1.call-update) | async-done | bytes 116752
  525.6 107.6 %reduce-scatter.8.cloned.1.call-done = bf16[96,768]{1,0:T(8,128)(2,1)} async-done(((bf16[3072,768]{1,0:T(8,128)(2,1)}), bf16[96,768]{1,0:T(8,128)(2,1)}) %reduce-scatter.8.cloned.1.call-update) | async-done | bytes 147472 | tf_op jit(solution)/shard_map/reduce_scatter | solution.py:173
  634.8 116.1 %reduce-scatter.6.cloned.1.call-done = bf16[24,3840]{1,0:T(8,128)(2,1)} async-done(((bf16[768,3840]{1,0:T(8,128)(2,1)}), bf16[24,3840]{1,0:T(8,128)(2,1)}) %reduce-scatter.6.cloned.1.call-update) | async-done | bytes 184336 | tf_op jit(solution)/shard_map/reduce_scatter | solution.py:185
  (232 shorter events, 123.8 us)
Async XLA Ops:
  7.2 18.1 %copy-start.56 = (s32[1,2]{1,0:T(1,128)S(1)}, s32[1,2]{1,0:T(1,128)}, u32[]{:S(2)}) copy-start(s32[1,2]{1,0:T(1,128)} %param.34) | copy-start | bytes 28
  7.2 20.0 %copy-start = (bf16[1,2,512,768]{3,2,1,0:T(8,128)(2,1)S(1)}, bf16[1,2,512,768]{3,2,1,0:T(8,128)(2,1)}, u32[]{:S(2)}) copy-start(bf16[1,2,512,768]{3,2,1,0:T(8,128)(2,1)} %param.35) | copy-start | bytes 4718596
  7.2 72.9 %all-gather.4.cloned.1.call-start = ((), (), s32[]{:S(2)}) async-start(), calls=%async_computation.3 | async-start | bytes 3852288 | tf_op jit(solution)/shard_map/all_gather | solution.py:127
  15.7 163.9 %all-gather.6.cloned.1.call-start = ((), (), s32[]{:S(2)}) async-start(), calls=%async_computation.4 | async-start | bytes 6082560 | tf_op jit(solution)/shard_map/all_gather | solution.py:133
  17.4 197.8 %all-gather.8.cloned.1.call-start = ((), (), s32[]{:S(2)}) async-start(), calls=%async_computation.5 | async-start | bytes 4866048 | tf_op jit(solution)/shard_map/all_gather | solution.py:136
  19.1 44.5 %copy-start.21 = (bf16[1,2,512,768]{2,3,1,0:T(8,128)(2,1)}, bf16[1,2,512,768]{2,3,1,0:T(8,128)(2,1)S(1)}, u32[]{:S(2)}) copy-start(bf16[1,2,512,768]{2,3,1,0:T(8,128)(2,1)S(1)} %copy.104) | copy-start | bytes 4718596
  19.2 41.0 %collective-permute-start = (bf16[2,512,768]{1,2,0:T(8,128)(2,1)S(1)}, bf16[2,512,768]{1,2,0:T(8,128)(2,1)}, u32[]{:S(2)}, u32[]{:S(2)}) collective-permute-start(bf16[2,512,768]{1,2,0:T(8,128)(2,1)S(1)} %bitcast.126), channel_id=1, source_target_pairs={{0,16},{1,17},{2,18},{3,19},{4,20},{5,21},{6,22},{7,23},{8,24},{9,... | collective-permute-start | bytes 4718600 | tf_op jit(solution)/shard_map/ppermute | solution.py:104
  25.2 495.7 %reduce-scatter.10.cloned.1.call-start = ((), (), s32[]{:S(2)}) async-start(), calls=%async_computation.8 | async-start | bytes 3852288
  68.5 15.1 %copy-start.31 = (bf16[1,2,512,768]{3,2,1,0:T(8,128)(2,1)S(1)}, bf16[1,2,512,768]{3,2,1,0:T(8,128)(2,1)}, u32[]{:S(2)}) copy-start(bf16[1,2,512,768]{3,2,1,0:T(8,128)(2,1)} %param.18) | copy-start | bytes 4718596
  97.6 12.8 %copy-start.1 = (bf16[1,1024,768]{1,2,0:T(8,128)(2,1)}, bf16[1,1024,768]{1,2,0:T(8,128)(2,1)S(1)}, u32[]{:S(2)}) copy-start(bf16[1,1024,768]{1,2,0:T(8,128)(2,1)S(1)} %copy.117) | copy-start | bytes 4718596
  97.6 12.8 %copy-start.3 = (pred[512,1024]{1,0:T(8,128)(4,1)S(1)}, pred[512,1024]{1,0:T(8,128)(4,1)}, u32[]{:S(2)}) copy-start(pred[512,1024]{1,0:T(8,128)(4,1)} %get-tuple-element.56) | copy-start | bytes 1572868
  110.4 12.5 %copy-start.41 = (f32[12,512]{1,0:T(8,128)}, f32[12,512]{1,0:T(8,128)S(1)}, u32[]{:S(2)}) copy-start(f32[12,512]{1,0:T(8,128)S(1)} %get-tuple-element.59) | copy-start | bytes 73732
  130.7 24.6 %copy-start.37 = (f32[12,512]{1,0:T(8,128)}, f32[12,512]{1,0:T(8,128)S(1)}, u32[]{:S(2)}) copy-start(f32[12,512]{1,0:T(8,128)S(1)} %log_add_fusion) | copy-start | bytes 73732
  130.8 12.4 %copy-start.7 = (pred[512,1024]{1,0:T(8,128)(4,1)S(1)}, pred[512,1024]{1,0:T(8,128)(4,1)}, u32[]{:S(2)}) copy-start(pred[512,1024]{1,0:T(8,128)(4,1)} %get-tuple-element.55) | copy-start | bytes 1572868
  143.2 12.2 %copy-start.4 = (pred[512,1024]{1,0:T(8,128)(4,1)S(1)}, pred[512,1024]{1,0:T(8,128)(4,1)}, u32[]{:S(2)}) copy-start(pred[512,1024]{1,0:T(8,128)(4,1)} %get-tuple-element.56) | copy-start | bytes 1572868
  143.2 12.2 %copy-start.14 = (bf16[1,1024,768]{1,2,0:T(8,128)(2,1)S(1)}, bf16[1,1024,768]{1,2,0:T(8,128)(2,1)}, u32[]{:S(2)}) copy-start(bf16[1,1024,768]{1,2,0:T(8,128)(2,1)} %copy.116) | copy-start | bytes 4718596
  155.3 12.3 %copy-start.39 = (f32[12,512]{1,0:T(8,128)}, f32[12,512]{1,0:T(8,128)S(1)}, u32[]{:S(2)}) copy-start(f32[12,512]{1,0:T(8,128)S(1)} %log_add_fusion.1) | copy-start | bytes 73732
  155.4 12.2 %copy-start.16 = (bf16[1,1024,768]{1,2,0:T(8,128)(2,1)S(1)}, bf16[1,1024,768]{1,2,0:T(8,128)(2,1)}, u32[]{:S(2)}) copy-start(bf16[1,1024,768]{1,2,0:T(8,128)(2,1)} %copy.114) | copy-start | bytes 4718596
  167.6 12.0 %copy-start.53 = (f32[768]{0:T(1024)S(1)}, f32[768]{0:T(1024)}, u32[]{:S(2)}) copy-start(f32[768]{0:T(1024)} %get-tuple-element.28) | copy-start | bytes 9220
  185.4 29.8 %copy-start.52 = (f32[768]{0:T(1024)S(1)}, f32[768]{0:T(1024)}, u32[]{:S(2)}) copy-start(f32[768]{0:T(1024)} %get-tuple-element.25) | copy-start | bytes 9220
  228.5 16.7 %slice-start.2 = ((s8[5898240]{0:T(1024)(128)(4,1)}), s8[4194304]{0:T(1024)(128)(4,1)S(1)}, s32[]{:S(2)}) async-start(s8[5898240]{0:T(1024)(128)(4,1)} %bitcast.156), calls=%async_computation.11 | async-start | bytes 8388608
  230.3 14.9 %copy-start.27 = (f32[1024,768]{1,0:T(8,128)}, f32[1024,768]{1,0:T(8,128)S(1)}, u32[]{:S(2)}) copy-start(f32[1024,768]{1,0:T(8,128)S(1)} %get-tuple-element.40) | copy-start | bytes 9437188
  230.3 14.9 %copy-start.10 = (f32[1024,768]{1,0:T(8,128)S(1)}, f32[1024,768]{1,0:T(8,128)}, u32[]{:S(2)}) copy-start(f32[1024,768]{1,0:T(8,128)} %copy-done.9) | copy-start | bytes 9437188
  230.3 14.9 %slice-start.3 = ((s8[5898240]{0:T(1024)(128)(4,1)}), s8[1703936]{0:T(1024)(128)(4,1)S(1)}, s32[]{:S(2)}) async-start(s8[5898240]{0:T(1024)(128)(4,1)} %bitcast.156), calls=%async_computation.12 | async-start | bytes 3407872
  321.7 12.9 %copy-start.6 = (pred[512,1024]{1,0:T(8,128)(4,1)S(1)}, pred[512,1024]{1,0:T(8,128)(4,1)}, u32[]{:S(2)}) copy-start(pred[512,1024]{1,0:T(8,128)(4,1)} %get-tuple-element.56) | copy-start | bytes 1572868
  321.8 12.9 %copy-start.15 = (bf16[1,1024,768]{1,2,0:T(8,128)(2,1)S(1)}, bf16[1,1024,768]{1,2,0:T(8,128)(2,1)}, u32[]{:S(2)}) copy-start(bf16[1,1024,768]{1,2,0:T(8,128)(2,1)} %copy.116) | copy-start | bytes 4718596
  321.8 12.9 %copy-start.30 = (bf16[512,768]{0,1:T(8,128)(2,1)S(1)}, bf16[512,768]{0,1:T(8,128)(2,1)}, u32[]{:S(2)}) copy-start(bf16[512,768]{0,1:T(8,128)(2,1)} %get-tuple-element.49) | copy-start | bytes 2359300
  422.1 211.1 %reduce-scatter.8.cloned.1.call-start = ((), (), s32[]{:S(2)}) async-start(), calls=%async_computation.7 | async-start | bytes 4866048 | tf_op jit(solution)/shard_map/reduce_scatter | solution.py:173
  433.9 316.9 %reduce-scatter.6.cloned.1.call-start = ((), (), s32[]{:S(2)}) async-start(), calls=%async_computation.6 | async-start | bytes 6082560 | tf_op jit(solution)/shard_map/reduce_scatter | solution.py:185
  455.2 9.4 %copy-start.33 = (bf16[12,64,512]{2,1,0:T(8,128)(2,1)S(1)}, bf16[12,64,512]{2,1,0:T(8,128)(2,1)}, u32[]{:S(2)}) copy-start(bf16[12,64,512]{2,1,0:T(8,128)(2,1)} %get-tuple-element.75) | copy-start | bytes 2359300
  455.2 9.5 %copy-start.34 = (bf16[12,64,512]{2,1,0:T(8,128)(2,1)S(1)}, bf16[12,64,512]{2,1,0:T(8,128)(2,1)}, u32[]{:S(2)}) copy-start(bf16[12,64,512]{2,1,0:T(8,128)(2,1)} %get-tuple-element.77) | copy-start | bytes 2359300
  463.3 41.9 %collective-permute-start.1 = (bf16[2,512,768]{2,1,0:T(8,128)(2,1)S(1)}, bf16[2,512,768]{2,1,0:T(8,128)(2,1)S(1)}, u32[]{:S(2)}, u32[]{:S(2)}) collective-permute-start(bf16[2,512,768]{2,1,0:T(8,128)(2,1)S(1)} %slice.274), channel_id=1, source_target_pairs={{16,0},{17,1},{18,2},{19,3},{20,4},{21,5},{22,6},{23,7},{24,8},{25... | collective-permute-start | bytes 4718600 | tf_op jit(solution)/shard_map/ppermute | solution.py:227
  (39 other events, 184.8 us)
Sparse Core Ops, SparseCore 0:
  15.8 64.2 all-gather.3
  83.6 66.3 all-gather.5
  152.8 62.2 all-gather.7
  422.2 98.7 reduce-scatter.9
  526.3 106.8 reduce-scatter.7
  638.6 112.1 reduce-scatter.5
where the time goes:
time: 765 us; the launch traced here: 761 us
  waiting for transfers between devices  336 us (44%)
  matrix products  242 us (32%)
  other arithmetic  90.9 us (12%)
  local copies, waits for them, and re-layouts  68 us (9%)
  between operations  16.4 us (2%)
    reduce_scatter x1, waiting for transfers between devices, on_device(): lax.psum_scatter(jnp.concatenate([g_output, g_inner], axis=1).astype(BF16...  116 us
    reduce_scatter x1, waiting for transfers between devices, on_device(): lax.psum_scatter(g_outer, BOTH, scatter_dimension=0, tiled=True).astype(F32)  108 us
    dot_general x2, matrix products, attend_back(): jnp.einsum('qhd,khd->hqk', grad_h, heads_of(v), preferred_element_type=F32)  43.2 us
    ppermute x1, waiting for transfers between devices, on_device(): lax.ppermute(via_kv[:, rows:].astype(BF16), 'seq', [(1, 0)]).astype(F32)  37.9 us
    dot_general x5, matrix products, dot_t(): lax.dot_general(a, b, (((1,), (1,)), ((), ())), preferred_element_type=F32)  35.8 us
    dot_general x5, matrix products, t_dot(): lax.dot_general(a, b, (((0,), (0,)), ((), ())), preferred_element_type=F32)  35.6 us
    convert_element_type x2, other arithmetic, attend_back(): grad_scores = (probs * (grad_probs - row_dot)).astype(BF16)  35.1 us
    dot_general x5, matrix products, dot(): return jnp.dot(a, b, preferred_element_type=F32)  30.3 us
  transfers between devices with their start and end apart: 8, of which 7 were waited for; matrix products, arithmetic and copies ran while one was open for 23% of the time, Pallas kernels for 0%

commit v1 on v0

--- a/solution.py
+++ b/solution.py
@@ -133,7 +133,8 @@
     second_pack = lax.all_gather(
         jnp.concatenate([output_weight, inner_weight], axis=1), BOTH, axis=0, tiled=True
     )
-    full_outer = lax.all_gather(outer_weight, BOTH, axis=0, tiled=True)
+    copies = jnp.concatenate([outer_weight] * lax.axis_size(BOTH), axis=0)
+    full_outer = lax.all_to_all(copies, BOTH, 0, 0, tiled=True)
     full_query = first_pack[:, :width]
     full_kv = first_pack[:, width : 3 * width]
     small_all = first_pack[:, 3 * width : 3 * width + small_count].astype(F32)

time: 765 us -> 789 us (1.031)
  waiting for transfers between devices: 336 us -> 350 us
    all_gather x1 -> x0, waiting for transfers between devices: 19.7 us -> none  [on_device(): full_outer = lax.all_gather(outer_weight, BOTH, axis=0, tiled=True)]
    ppermute x1, waiting for transfers between devices: 30.2 us -> 49.9 us  [on_device(): before = lax.ppermute(x, 'seq', [(0, 1)])]
    unnamed x7 -> x6, waiting for transfers between devices: 13.4 us -> 18.5 us
  transfers between devices with their start and end apart: 8 -> 8, of which waited for: 7 -> 6; matrix products, arithmetic and copies ran while one was open for 23% -> 23% of each run, Pallas kernels for 0% -> 0%
where the time goes in v1:
time: 789 us; the launch traced here: 785 us
  waiting for transfers between devices  350 us (44%)
  matrix products  244 us (31%)
  other arithmetic  90 us (11%)
  local copies, waits for them, and re-layouts  71.3 us (9%)
  between operations  16.3 us (2%)
  starting transfers between devices  12.6 us (2%)
    reduce_scatter x1, waiting for transfers between devices, on_device(): lax.psum_scatter(jnp.concatenate([g_output, g_inner], axis=1).astype(BF16...  116 us
    reduce_scatter x1, waiting for transfers between devices, on_device(): lax.psum_scatter(g_outer, BOTH, scatter_dimension=0, tiled=True).astype(F32)  107 us
    ppermute x1, waiting for transfers between devices, on_device(): before = lax.ppermute(x, 'seq', [(0, 1)])  49.9 us
    dot_general x2, matrix products, attend_back(): jnp.einsum('qhd,khd->hqk', grad_h, heads_of(v), preferred_element_type=F32)  43.2 us
    ppermute x1, waiting for transfers between devices, on_device(): lax.ppermute(via_kv[:, rows:].astype(BF16), 'seq', [(1, 0)]).astype(F32)  40.9 us
    dot_general x5, matrix products, dot_t(): lax.dot_general(a, b, (((1,), (1,)), ((), ())), preferred_element_type=F32)  36.2 us
    dot_general x5, matrix products, t_dot(): lax.dot_general(a, b, (((0,), (0,)), ((), ())), preferred_element_type=F32)  36.1 us
    convert_element_type x2, other arithmetic, attend_back(): grad_scores = (probs * (grad_probs - row_dot)).astype(BF16)  35.1 us
  transfers between devices with their start and end apart: 8, of which 6 were waited for; matrix products, arithmetic and copies ran while one was open for 23% of the time, Pallas kernels for 0%

profile of v1, /device:TPU:0, one launch (start us, length us, event | category | flops | bytes accessed | tf_op | source)
XLA Modules:
  0.0 784.9 jit_solution(10241211123313909443)
XLA Ops:
  17.3 6.1 collective-permute-start
  29.8 5.0 all-to-all-start
  40.4 49.9 %collective-permute-done = bf16[2,512,768]{1,2,0:T(8,128)(2,1)} collective-permute-done((bf16[2,512,768]{1,2,0:T(8,128)(2,1)S(1)}, bf16[2,512,768]{1,2,0:T(8,128)(2,1)}, u32[]{:S(2)}, u32[]{:S(2)}) %collective-permute-start) | collective-permute-done | bytes 1572896 | tf_op jit(solution)/shard_map/ppermute | solution.py:104
  98.6 17.9 %all-gather.3.cloned.1.call-done = bf16[768,2432]{1,0:T(8,128)(2,1)} async-done(((bf16[24,2432]{1,0:T(8,128)(2,1)}), bf16[768,2432]{1,0:T(8,128)(2,1)}) %all-gather.3.cloned.1.call-update) | async-done | bytes 3735568 | tf_op jit(solution)/shard_map/all_gather | solution.py:127
  119.5 7.4 add_convert_fusion
  136.4 10.6 %fusion.1 = (f32[12,512]{1,0:T(8,128)S(1)}, f32[12,512,1024]{2,1,0:T(8,128)}) fusion(pred[512,1024]{1,0:T(8,128)(4,1)S(1)} %copy-done.4, bf16[512,12,64]{0,2,1:T(8,128)(2,1)S(1)} %bitcast.117, bf16[1024,12,64]{0,2,1:T(8,128)(2,1)S(1)} %bitcast.113), kind=kOutput, calls=%fused_computation.11 | convolution fusion | flops 824174592 | bytes 28073984 | tf_op jit(solution)/shard_map/qhd,khd->hqk/dot_general | solution.py:46
  147.0 12.4 %exponential_reduce_fusion = f32[12,512]{1,0:T(8,128)} fusion(f32[12,512,1024]{2,1,0:T(8,128)} %get-tuple-element.60, f32[12,512]{1,0:T(8,128)S(1)} %get-tuple-element.59, pred[512,1024]{1,0:T(8,128)(4,1)S(1)} %copy-done.4), kind=kLoop, calls=%fused_computation.5 | loop fusion | flops 25159680 | bytes 25739264 | tf_op jit(solution)/shard_map/reduce_sum | solution.py:50
  167.4 12.7 %fusion = (f32[12,512]{1,0:T(8,128)S(1)}, f32[12,512,1024]{2,1,0:T(8,128)}) fusion(pred[512,1024]{1,0:T(8,128)(4,1)} %get-tuple-element.55, bf16[512,12,64]{0,2,1:T(8,128)(2,1)} %bitcast.119, bf16[1024,12,64]{0,2,1:T(8,128)(2,1)S(1)} %bitcast.115), kind=kOutput, calls=%fused_computation.10 | convolution fusion | flops 824174592 | bytes 28073984 | tf_op jit(solution)/shard_map/qhd,khd->hqk/dot_general | solution.py:46
  180.1 12.2 %exponential_reduce_fusion.1 = f32[12,512]{1,0:T(8,128)S(1)} fusion(f32[12,512,1024]{2,1,0:T(8,128)} %get-tuple-element.62, f32[12,512]{1,0:T(8,128)S(1)} %get-tuple-element.61, pred[512,1024]{1,0:T(8,128)(4,1)S(1)} %copy-done.8), kind=kLoop, calls=%fused_computation.8 | loop fusion | flops 25159680 | bytes 25739264 | tf_op jit(solution)/shard_map/reduce_sum | solution.py:50
  192.4 12.1 %convolution_convert_fusion.7 = bf16[12,64,512]{2,1,0:T(8,128)(2,1)} fusion(bf16[1024,12,64]{0,2,1:T(8,128)(2,1)S(1)} %bitcast.123, f32[12,512,1024]{2,1,0:T(8,128)} %get-tuple-element.60, f32[12,512]{1,0:T(8,128)S(1)} %log_add_fusion, pred[512,1024]{1,0:T(8,128)(4,1)S(1)} %copy-done.5), kind=kOutput, calls=%fused_computation.85 | convolution fusion | flops 830865408 | bytes 28073984 | tf_op jit(solution)/shard_map/hqk,khd->qhd/dot_general | solution.py:53
  204.4 11.9 %convolution_convert_fusion.8 = bf16[12,64,512]{2,1,0:T(8,128)(2,1)} fusion(bf16[1024,12,64]{0,2,1:T(8,128)(2,1)S(1)} %bitcast.125, f32[12,512,1024]{2,1,0:T(8,128)} %get-tuple-element.62, f32[12,512]{1,0:T(8,128)S(1)} %log_add_fusion.1, pred[512,1024]{1,0:T(8,128)(4,1)S(1)} %copy-done.8), kind=kOutput, calls=%fused_computation.86 | convolution fusion | flops 830865408 | bytes 28073984 | tf_op jit(solution)/shard_map/hqk,khd->qhd/dot_general | solution.py:53
  222.1 10.1 %multiply_convert_fusion.2 = (bf16[1024,3072]{1,0:T(8,128)(2,1)}, f32[1024,3072]{1,0:T(8,128)}) fusion(f32[3072]{0:T(1024)S(1)} %add.172, bf16[768,3840]{1,0:T(8,128)(2,1)S(1)} %copy-done.57, f32[1024,768]{1,0:T(8,128)S(1)} %get-tuple-element.64, f32[768]{0:T(1024)S(1)} %copy-done.51, f32[768]{0:T(1024)S(1)} %get-tuple-element.27, ...), kind=kOutput, calls=%fused_computation.21 | convolution fusion | flops 4854644736 | bytes 26767360 | tf_op jit(solution)/shard_map/dot_general | solution.py:16
  232.2 9.3 %fusion.72 = (f32[1024]{0:T(1024)S(1)}, f32[1024,768]{1,0:T(8,128)S(1)}) fusion(f32[768]{0:T(1024)S(1)} %copy-done.53, bf16[1024,3072]{1,0:T(8,128)(2,1)} %get-tuple-element.65, bf16[3072,768]{1,0:T(8,128)(2,1)} %bitcast.26, f32[768]{0:T(1024)S(1)} %copy-done.51, f32[768]{0:T(1024)S(1)} %get-tuple-element.27, f32[1024]{0:T(1024)S(1)} %add_rsqrt_fusion.1, ...), kind=kOutput, calls=%fused_computation.187 | convolution fusion | flops 4837342208 | bytes 17323008 | tf_op jit(solution)/shard_map/dot_general | solution.py:16
  247.2 15.4 %fusion.73 = (bf16[3072]{0:T(1024)(128)(2,1)}, bf16[1024,3072]{1,0:T(8,128)(2,1)}) fusion(f32[1024,3072]{1,0:T(8,128)} %get-tuple-element.66, f32[3072]{0:T(1024)S(1)} %add.172, bf16[3072,768]{1,0:T(8,128)(2,1)} %bitcast.26, f32[1024,768]{1,0:T(8,128)S(1)} %get-tuple-element.40), kind=kOutput, calls=%fused_computation.188 | convolution fusion | flops 4876661760 | bytes 26757120 | tf_op jit(solution)/shard_map/dot_general | solution.py:20
  262.6 8.8 %multiply_reduce_fusion.2 = (bf16[768]{0:T(1024)(128)(2,1)}, f32[1024]{0:T(1024)S(1)}, f32[1024]{0:T(1024)S(1)}, bf16[768]{0:T(1024)(128)(2,1)}, f32[1024,768]{1,0:T(8,128)S(1)}) fusion(f32[1024,768]{1,0:T(8,128)S(1)} %copy-done.11, f32[1024]{0:T(1024)S(1)} %add_rsqrt_fusion.1, f32[1024]{0:T(1024)S(1)} %broadcast_multiply_fusion.4, ...), kind=kOutput, calls=%fused_computation.52 | convolution fusion | flops 4839698432 | bytes 20470784 | tf_op jit(solution)/shard_map/dot_general | solution.py:20
  275.6 12.7 %convolution_convert_fusion.3 = bf16[12,64,1024]{2,1,0:T(8,128)(2,1)} fusion(bf16[512,12,64]{0,2,1:T(8,128)(2,1)S(1)} %bitcast.136, f32[12,512,1024]{2,1,0:T(8,128)} %get-tuple-element.62, f32[12,512]{1,0:T(8,128)S(1)} %copy-done.40, pred[512,1024]{1,0:T(8,128)(4,1)S(1)} %copy-done.9), kind=kOutput, calls=%fused_computation.75 | convolution fusion | flops 831258624 | bytes 28073984 | tf_op jit(solution)/shard_map/hqk,qhd->khd/dot_general | solution.py:65
  288.3 21.9 %multiply_reduce_fusion.1 = (f32[12,512]{1,0:T(8,128)}, f32[12,512,1024]{2,1,0:T(8,128)}) fusion(f32[12,512,1024]{2,1,0:T(8,128)} %get-tuple-element.62, f32[12,512]{1,0:T(8,128)S(1)} %copy-done.40, pred[512,1024]{1,0:T(8,128)(4,1)S(1)} %copy-done.9, bf16[512,12,64]{0,2,1:T(8,128)(2,1)S(1)} %bitcast.137, bf16[1024,12,64]{0,2,1:T(8,128)(2,1)S(1)} %bitcast.126), kind=kOutput, calls=%fused_computation.3 | convolution fusion | flops 836757504 | bytes 53264384 | tf_op jit(solution)/shard_map/qhd,khd->hqk/dot_general | solution.py:60
  310.2 17.5 %multiply_convert_fusion.1 = bf16[12,512,1024]{2,1,0:T(8,128)(2,1)S(1)} fusion(f32[12,512,1024]{2,1,0:T(8,128)} %get-tuple-element.73, f32[12,512,1024]{2,1,0:T(8,128)} %get-tuple-element.62, f32[12,512]{1,0:T(8,128)} %get-tuple-element.72, f32[12,512]{1,0:T(8,128)} %copy-done.39, pred[512,1024]{1,0:T(8,128)(4,1)} %get-tuple-element.55), kind=kLoop, calls=%fused_computation.2 | loop fusion | flops 37748736 | bytes 63488000 | tf_op jit(solution)/shard_map/convert_element_type | solution.py:62
  327.8 6.2 bitcast_reduce_fusion.1
  338.7 12.8 %convolution_convert_fusion.2 = bf16[12,64,1024]{2,1,0:T(8,128)(2,1)} fusion(bf16[512,12,64]{0,2,1:T(8,128)(2,1)S(1)} %bitcast.134, f32[12,512,1024]{2,1,0:T(8,128)} %get-tuple-element.60, f32[12,512]{1,0:T(8,128)S(1)} %copy-done.38, pred[512,1024]{1,0:T(8,128)(4,1)S(1)} %copy-done.6), kind=kOutput, calls=%fused_computation.74 | convolution fusion | flops 831258624 | bytes 28073984 | tf_op jit(solution)/shard_map/hqk,qhd->khd/dot_general | solution.py:65
  351.6 21.3 %multiply_reduce_fusion = (f32[12,512]{1,0:T(8,128)S(1)}, f32[12,512,1024]{2,1,0:T(8,128)}) fusion(f32[12,512,1024]{2,1,0:T(8,128)} %get-tuple-element.60, f32[12,512]{1,0:T(8,128)S(1)} %copy-done.38, pred[512,1024]{1,0:T(8,128)(4,1)S(1)} %copy-done.7, bf16[512,12,64]{0,2,1:T(8,128)(2,1)S(1)} %bitcast.135, bf16[1024,12,64]{0,2,1:T(8,128)(2,1)S(1)} %bitcast.124), kind=kOutput, calls=%fused_computation.1 | convolution fusion | flops 836757504 | bytes 53264384 | tf_op jit(solution)/shard_map/qhd,khd->hqk/dot_general | solution.py:60
  372.9 17.6 %multiply_convert_fusion = bf16[12,512,1024]{2,1,0:T(8,128)(2,1)S(1)} fusion(f32[12,512,1024]{2,1,0:T(8,128)} %get-tuple-element.71, f32[12,512,1024]{2,1,0:T(8,128)} %get-tuple-element.60, f32[12,512]{1,0:T(8,128)S(1)} %get-tuple-element.70, f32[12,512]{1,0:T(8,128)S(1)} %copy-done.38, pred[512,1024]{1,0:T(8,128)(4,1)} %get-tuple-element.56), kind=kLoop, calls=%fused_computation | loop fusion | flops 37748736 | bytes 63488000 | tf_op jit(solution)/shard_map/convert_element_type | solution.py:62
  390.5 6.2 bitcast_reduce_fusion
  429.3 8.0 %bitcast_convert_fusion = bf16[768,1536]{1,0:T(8,128)(2,1)S(1)} fusion(bf16[2,512,768]{1,2,0:T(8,128)(2,1)} %collective-permute-done, bf16[2,512,768]{1,2,0:T(8,128)(2,1)} %bitcast.130, bf16[1,1024,768]{2,1,0:T(8,128)(2,1)S(1)} %copy-done.19, bf16[1,1024,768]{2,1,0:T(8,128)(2,1)S(1)} %copy-done.21, bf16[1,1024,768]{2,1,0:T(8,128)(2,1)} %copy.119, ...), kind=kOutput, calls=%fused_computation.30 | convolution fusion | flops 4864475136 | bytes 11796480 | tf_op jit(solution)/shard_map/dot_general | solution.py:24
  440.5 9.8 %convolution_convert_fusion = bf16[3072,768]{1,0:T(8,128)(2,1)} fusion(bf16[1024,3072]{1,0:T(8,128)(2,1)} %get-tuple-element.65, f32[1024,768]{1,0:T(8,128)S(1)} %copy-done.30), kind=kOutput, calls=%fused_computation.28 | convolution fusion | flops 4834983936 | bytes 14155776 | tf_op jit(solution)/shard_map/dot_general | solution.py:24
  450.4 5.1 convolution_convert_fusion.5
  458.1 8.7 %convolution_convert_fusion.1 = bf16[768,3072]{1,0:T(8,128)(2,1)S(1)} fusion(bf16[1024,3072]{1,0:T(8,128)(2,1)} %get-tuple-element.79, f32[1024,768]{1,0:T(8,128)S(1)} %copy-done.12, f32[768]{0:T(1024)S(1)} %copy-done.52, f32[768]{0:T(1024)S(1)} %get-tuple-element.27, f32[1024]{0:T(1024)S(1)} %add_rsqrt_fusion.1, f32[1024]{0:T(1024)S(1)} %broadcast_multiply_fusion.4), kind=kOutput, calls=%fused_computation.29 | convolution fusion | flops 4838129664 | bytes 14170112 | tf_op jit(solution)/shard_map/dot_general | solution.py:24
  471.7 8.0 %fusion.26 = f32[2,1024,768]{2,1,0:T(8,128)S(1)} fusion(bf16[768,2432]{1,0:T(8,128)(2,1)} %all-gather.3.cloned.1.call-done, bf16[1,1024,768]{2,1,0:T(8,128)(2,1)S(1)} %copy-done.20, bf16[1,1024,768]{2,1,0:T(8,128)(2,1)S(1)} %copy-done.22, bf16[1,1024,768]{2,1,0:T(8,128)(2,1)} %copy.119, bf16[1,1024,768]{2,1,0:T(8,128)(2,1)} %copy.118), kind=kOutput, calls=%fused_computation.68 | convolution fusion | flops 4857004032 | bytes 14942208 | tf_op jit(solution)/shard_map/dot_general | solution.py:20
  483.9 40.9 %collective-permute-done.1 = bf16[2,512,768]{2,1,0:T(8,128)(2,1)S(1)} collective-permute-done((bf16[2,512,768]{2,1,0:T(8,128)(2,1)S(1)}, bf16[2,512,768]{2,1,0:T(8,128)(2,1)S(1)}, u32[]{:S(2)}, u32[]{:S(2)}) %collective-permute-start.1) | collective-permute-done | bytes 1572896 | tf_op jit(solution)/shard_map/ppermute | solution.py:228
  527.2 18.4 %reduce-scatter.10.cloned.1.call-done = bf16[24,2432]{1,0:T(8,128)(2,1)} async-done(((bf16[768,2432]{1,0:T(8,128)(2,1)}), bf16[24,2432]{1,0:T(8,128)(2,1)}) %reduce-scatter.10.cloned.1.call-update) | async-done | bytes 116752
  550.2 107.3 %reduce-scatter.8.cloned.1.call-done = bf16[96,768]{1,0:T(8,128)(2,1)} async-done(((bf16[3072,768]{1,0:T(8,128)(2,1)}), bf16[96,768]{1,0:T(8,128)(2,1)}) %reduce-scatter.8.cloned.1.call-update) | async-done | bytes 147472 | tf_op jit(solution)/shard_map/reduce_scatter | solution.py:174
  659.1 116.0 %reduce-scatter.6.cloned.1.call-done = bf16[24,3840]{1,0:T(8,128)(2,1)} async-done(((bf16[768,3840]{1,0:T(8,128)(2,1)}), bf16[24,3840]{1,0:T(8,128)(2,1)}) %reduce-scatter.6.cloned.1.call-update) | async-done | bytes 184336 | tf_op jit(solution)/shard_map/reduce_scatter | solution.py:186
  (255 shorter events, 128.4 us)
Async XLA Ops:
  7.2 19.9 %copy-start = (bf16[96,768]{1,0:T(8,128)(2,1)S(1)}, bf16[96,768]{1,0:T(8,128)(2,1)}, u32[]{:S(2)}) copy-start(bf16[96,768]{1,0:T(8,128)(2,1)} %param.30) | copy-start | bytes 442372
  7.2 109.3 %all-gather.3.cloned.1.call-start = ((), (), s32[]{:S(2)}) async-start(), calls=%async_computation.4 | async-start | bytes 3852288 | tf_op jit(solution)/shard_map/all_gather | solution.py:127
  17.3 73.0 %copy-start.23 = (bf16[1,2,512,768]{2,3,1,0:T(8,128)(2,1)}, bf16[1,2,512,768]{2,3,1,0:T(8,128)(2,1)S(1)}, u32[]{:S(2)}) copy-start(bf16[1,2,512,768]{2,3,1,0:T(8,128)(2,1)S(1)} %copy.104) | copy-start | bytes 4718596
  17.3 72.9 %collective-permute-start = (bf16[2,512,768]{1,2,0:T(8,128)(2,1)S(1)}, bf16[2,512,768]{1,2,0:T(8,128)(2,1)}, u32[]{:S(2)}, u32[]{:S(2)}) collective-permute-start(bf16[2,512,768]{1,2,0:T(8,128)(2,1)S(1)} %bitcast.128), channel_id=1, source_target_pairs={{0,16},{1,17},{2,18},{3,19},{4,20},{5,21},{6,22},{7,23},{8,24},{9,... | collective-permute-start | bytes 4718600 | tf_op jit(solution)/shard_map/ppermute | solution.py:104
  29.8 202.3 %all-to-all-start = ((bf16[32,96,768]{2,1,0:T(8,128)(2,1)}), bf16[32,96,768]{2,1,0:T(8,128)(2,1)}, u32[]{:S(2)}, u32[]{:S(2)}) async-start(bf16[32,96,768]{2,1,0:T(8,128)(2,1)} %bitcast.131), calls=%async_computation | async-start | bytes 9437184 | tf_op jit(solution)/shard_map/all_to_all | solution.py:137
  34.9 181.5 %all-gather.5.cloned.1.call-start = ((), (), s32[]{:S(2)}) async-start(), calls=%async_computation.5 | async-start | bytes 6082560 | tf_op jit(solution)/shard_map/all_gather | solution.py:133
  35.6 509.9 %reduce-scatter.10.cloned.1.call-start = ((), (), s32[]{:S(2)}) async-start(), calls=%async_computation.8 | async-start | bytes 3852288
  136.4 10.6 %copy-start.13 = (bf16[512,768]{0,1:T(8,128)(2,1)}, bf16[512,768]{0,1:T(8,128)(2,1)S(1)}, u32[]{:S(2)}) copy-start(bf16[512,768]{0,1:T(8,128)(2,1)S(1)} %get-tuple-element.51) | copy-start | bytes 2359300
  147.0 12.4 %copy-start.41 = (f32[12,512]{1,0:T(8,128)}, f32[12,512]{1,0:T(8,128)S(1)}, u32[]{:S(2)}) copy-start(f32[12,512]{1,0:T(8,128)S(1)} %get-tuple-element.59) | copy-start | bytes 73732
  161.6 18.5 %copy-start.3 = (bf16[1,1024,768]{1,2,0:T(8,128)(2,1)}, bf16[1,1024,768]{1,2,0:T(8,128)(2,1)S(1)}, u32[]{:S(2)}) copy-start(bf16[1,1024,768]{1,2,0:T(8,128)(2,1)S(1)} %copy.115) | copy-start | bytes 4718596
  167.3 25.0 %copy-start.37 = (f32[12,512]{1,0:T(8,128)}, f32[12,512]{1,0:T(8,128)S(1)}, u32[]{:S(2)}) copy-start(f32[12,512]{1,0:T(8,128)S(1)} %log_add_fusion) | copy-start | bytes 73732
  167.4 12.7 %copy-start.8 = (pred[512,1024]{1,0:T(8,128)(4,1)S(1)}, pred[512,1024]{1,0:T(8,128)(4,1)}, u32[]{:S(2)}) copy-start(pred[512,1024]{1,0:T(8,128)(4,1)} %get-tuple-element.55) | copy-start | bytes 1572868
  180.1 12.3 %copy-start.5 = (pred[512,1024]{1,0:T(8,128)(4,1)S(1)}, pred[512,1024]{1,0:T(8,128)(4,1)}, u32[]{:S(2)}) copy-start(pred[512,1024]{1,0:T(8,128)(4,1)} %get-tuple-element.56) | copy-start | bytes 1572868
  180.1 12.3 %copy-start.16 = (bf16[1,1024,768]{1,2,0:T(8,128)(2,1)S(1)}, bf16[1,1024,768]{1,2,0:T(8,128)(2,1)}, u32[]{:S(2)}) copy-start(bf16[1,1024,768]{1,2,0:T(8,128)(2,1)} %copy.116) | copy-start | bytes 4718596
  192.3 12.1 %copy-start.39 = (f32[12,512]{1,0:T(8,128)}, f32[12,512]{1,0:T(8,128)S(1)}, u32[]{:S(2)}) copy-start(f32[12,512]{1,0:T(8,128)S(1)} %log_add_fusion.1) | copy-start | bytes 73732
  192.4 12.1 %copy-start.18 = (bf16[1,1024,768]{1,2,0:T(8,128)(2,1)S(1)}, bf16[1,1024,768]{1,2,0:T(8,128)(2,1)}, u32[]{:S(2)}) copy-start(bf16[1,1024,768]{1,2,0:T(8,128)(2,1)} %copy.114) | copy-start | bytes 4718596
  222.1 10.1 %copy-start.53 = (f32[768]{0:T(1024)S(1)}, f32[768]{0:T(1024)}, u32[]{:S(2)}) copy-start(f32[768]{0:T(1024)} %get-tuple-element.25) | copy-start | bytes 9220
  232.2 9.9 %copy-start.46 = (f32[768]{0:T(1024)S(1)}, f32[768]{0:T(1024)}, u32[]{:S(2)}) copy-start(f32[768]{0:T(1024)} %get-tuple-element.24) | copy-start | bytes 9220
  245.4 17.1 %slice-start = ((s8[5898240]{0:T(1024)(128)(4,1)}), s8[4194304]{0:T(1024)(128)(4,1)S(1)}, s32[]{:S(2)}) async-start(s8[5898240]{0:T(1024)(128)(4,1)} %bitcast.157), calls=%async_computation.9 | async-start | bytes 8388608
  247.2 15.4 %copy-start.29 = (f32[1024,768]{1,0:T(8,128)}, f32[1024,768]{1,0:T(8,128)S(1)}, u32[]{:S(2)}) copy-start(f32[1024,768]{1,0:T(8,128)S(1)} %get-tuple-element.40) | copy-start | bytes 9437188
  247.2 15.4 %copy-start.11 = (f32[1024,768]{1,0:T(8,128)S(1)}, f32[1024,768]{1,0:T(8,128)}, u32[]{:S(2)}) copy-start(f32[1024,768]{1,0:T(8,128)} %copy-done.10) | copy-start | bytes 9437188
  247.2 15.4 %slice-start.1 = ((s8[5898240]{0:T(1024)(128)(4,1)}), s8[1703936]{0:T(1024)(128)(4,1)S(1)}, s32[]{:S(2)}) async-start(s8[5898240]{0:T(1024)(128)(4,1)} %bitcast.157), calls=%async_computation.10 | async-start | bytes 3407872
  338.7 12.9 %copy-start.7 = (pred[512,1024]{1,0:T(8,128)(4,1)S(1)}, pred[512,1024]{1,0:T(8,128)(4,1)}, u32[]{:S(2)}) copy-start(pred[512,1024]{1,0:T(8,128)(4,1)} %get-tuple-element.56) | copy-start | bytes 1572868
  338.7 12.9 %copy-start.17 = (bf16[1,1024,768]{1,2,0:T(8,128)(2,1)S(1)}, bf16[1,1024,768]{1,2,0:T(8,128)(2,1)}, u32[]{:S(2)}) copy-start(bf16[1,1024,768]{1,2,0:T(8,128)(2,1)} %copy.116) | copy-start | bytes 4718596
  338.7 12.9 %copy-start.32 = (bf16[512,768]{0,1:T(8,128)(2,1)S(1)}, bf16[512,768]{0,1:T(8,128)(2,1)}, u32[]{:S(2)}) copy-start(bf16[512,768]{0,1:T(8,128)(2,1)} %get-tuple-element.49) | copy-start | bytes 2359300
  401.4 10.0 %copy-start.14 = (bf16[12,64,1024]{2,1,0:T(8,128)(2,1)S(1)}, bf16[12,64,1024]{2,1,0:T(8,128)(2,1)}, u32[]{:S(2)}) copy-start(bf16[12,64,1024]{2,1,0:T(8,128)(2,1)} %multiply_convert_fusion.4) | copy-start | bytes 4718596
  439.4 218.1 %reduce-scatter.8.cloned.1.call-start = ((), (), s32[]{:S(2)}) async-start(), calls=%async_computation.7 | async-start | bytes 4866048 | tf_op jit(solution)/shard_map/reduce_scatter | solution.py:174
  450.4 324.7 %reduce-scatter.6.cloned.1.call-start = ((), (), s32[]{:S(2)}) async-start(), calls=%async_computation.6 | async-start | bytes 6082560 | tf_op jit(solution)/shard_map/reduce_scatter | solution.py:186
  471.7 9.4 %copy-start.28 = (f32[1024,768]{1,0:T(8,128)S(1)}, f32[1024,768]{1,0:T(8,128)}, u32[]{:S(2)}) copy-start(f32[1024,768]{1,0:T(8,128)} %copy-done.27) | copy-start | bytes 9437188
  471.7 9.4 %copy-start.33 = (bf16[12,64,512]{2,1,0:T(8,128)(2,1)S(1)}, bf16[12,64,512]{2,1,0:T(8,128)(2,1)}, u32[]{:S(2)}) copy-start(bf16[12,64,512]{2,1,0:T(8,128)(2,1)} %get-tuple-element.75) | copy-start | bytes 2359300
  471.7 9.4 %copy-start.34 = (bf16[12,64,512]{2,1,0:T(8,128)(2,1)S(1)}, bf16[12,64,512]{2,1,0:T(8,128)(2,1)}, u32[]{:S(2)}) copy-start(bf16[12,64,512]{2,1,0:T(8,128)(2,1)} %get-tuple-element.77) | copy-start | bytes 2359300
  479.8 45.0 %collective-permute-start.1 = (bf16[2,512,768]{2,1,0:T(8,128)(2,1)S(1)}, bf16[2,512,768]{2,1,0:T(8,128)(2,1)S(1)}, u32[]{:S(2)}, u32[]{:S(2)}) collective-permute-start(bf16[2,512,768]{2,1,0:T(8,128)(2,1)S(1)} %slice.274), channel_id=1, source_target_pairs={{16,0},{17,1},{18,2},{19,3},{20,4},{21,5},{22,6},{23,7},{24,8},{25... | collective-permute-start | bytes 4718600 | tf_op jit(solution)/shard_map/ppermute | solution.py:228
  (36 other events, 197.0 us)
Sparse Core Ops, SparseCore 0:
  15.7 100.6 all-gather.2
  119.9 70.7 all-gather.4
  439.5 106.0 reduce-scatter.9
  550.9 106.5 reduce-scatter.7
  663.0 112.0 reduce-scatter.5
